TPU v7x, 8 devices: a whole 2x2x1 slice. The times are simulated.
8 devices in a mesh: dp: 1 (over z), tp: 8 (over y, x, core).
Axes of the slice: x: 2, y: 2, z: 1, core: 2. Of those that a mesh axis runs over, the one named last changes fastest.
Arguments:
- tokens: int32 [4], P('dp')
- lengths: int32 [4], P('dp')
- embed_table: bfloat16 [49152, 3840], P('tp')
- norm_gains: bfloat16 [9, 3840], replicated
- w_query: bfloat16 [2, 3840, 4096], P(None, None, 'tp')
- w_key: bfloat16 [2, 3840, 2048], P(None, None, 'tp')
- w_value: bfloat16 [2, 3840, 2048], P(None, None, 'tp')
- w_out: bfloat16 [2, 4096, 3840], P(None, 'tp')
- w_gate: bfloat16 [2, 3840, 15360], P(None, None, 'tp')
- w_up: bfloat16 [2, 3840, 15360], P(None, None, 'tp')
- w_down: bfloat16 [2, 15360, 3840], P(None, 'tp')
- key_local: bfloat16 [4, 1024, 8, 256], P('dp', None, 'tp')
- value_local: bfloat16 [4, 1024, 8, 256], P('dp', None, 'tp')
- key_global: bfloat16 [4, 4096, 8, 256], P('dp', None, 'tp')
- value_global: bfloat16 [4, 4096, 8, 256], P('dp', None, 'tp')
Outputs:
- output 1: float32 [4, 49152], P('dp', 'tp')
- output 2: bfloat16 [2, 4, 2048], P(None, 'dp', 'tp')
- output 3: bfloat16 [2, 4, 2048], P(None, 'dp', 'tp')
All inputs are finite; a program needn't handle non-finite values.
Results may differ from a plain program's by a relative error of at most 0.02.
Values are sent between devices in bfloat16 or wider.
A program may use at most 1 GiB of HBM per device.

v0:
```python
import math
import jax
import jax.numpy as jnp
from jax import lax
from jax.sharding import PartitionSpec as P


def rms_norm(hidden, gain):
    values = hidden.astype(jnp.float32)
    inv_rms = lax.rsqrt(jnp.mean(values * values, axis=-1, keepdims=True) + 1e-6)
    return (values * inv_rms * (1.0 + gain.astype(jnp.float32))).astype(jnp.bfloat16)


def rope_rotate(heads, lengths):
    head_dim = heads.shape[-1]
    half_dim = head_dim // 2
    inv_freq = 10000.0 ** (-2.0 * jnp.arange(half_dim, dtype=jnp.float32) / head_dim)
    angles = lengths.astype(jnp.float32)[:, None, None] * inv_freq
    cos_tab = jnp.cos(angles)
    sin_tab = jnp.sin(angles)
    lower_half = heads[..., :half_dim].astype(jnp.float32)
    upper_half = heads[..., half_dim:].astype(jnp.float32)
    return jnp.concatenate([lower_half * cos_tab - upper_half * sin_tab, upper_half * cos_tab + lower_half * sin_tab], axis=-1)


def write_slot(cache, rows, slots):
    def write_one(one_cache, one_row, one_slot):
        return lax.dynamic_update_slice(one_cache, one_row[None], (one_slot, 0, 0))
    return jax.vmap(write_one)(cache, rows, slots)


def cache_attention(queries, key_cache, value_cache, lengths, is_local):
    batch_size, slots_total, kv_heads, head_dim = key_cache.shape
    groups = queries.shape[1] // kv_heads
    grouped = queries.reshape(batch_size, kv_heads, groups, head_dim)
    scores = jnp.einsum("bkgd,bskd->bkgs", grouped, key_cache, preferred_element_type=jnp.float32)
    capped = 50.0 * jnp.tanh(scores / 50.0)
    slot_ids = jnp.arange(slots_total, dtype=jnp.int32)[None, :]
    valid_slots = slot_ids <= lengths[:, None]
    if is_local:
        valid_slots = valid_slots | (lengths[:, None] >= slots_total - 1)
    capped = jnp.where(valid_slots[:, None, None, :], capped, -1e30)
    attn_probs = jax.nn.softmax(capped, axis=-1).astype(jnp.bfloat16)
    attn_mixed = jnp.einsum("bkgs,bskd->bkgd", attn_probs, value_cache, preferred_element_type=jnp.float32)
    return attn_mixed.astype(jnp.bfloat16).reshape(batch_size, kv_heads * groups * head_dim)


def project(normed, weight):
    return jnp.dot(normed, weight, preferred_element_type=jnp.float32).astype(jnp.bfloat16)


def decoder_layer(hidden, lengths, layer_gains, weights, key_cache, value_cache, is_local):
    w_query, w_key, w_value, w_out, w_gate, w_up, w_down = weights
    batch_size, slots_total, kv_local, head_dim = key_cache.shape
    normed = rms_norm(hidden, layer_gains[0])
    queries = project(normed, w_query).reshape(batch_size, -1, head_dim)
    new_keys = project(normed, w_key).reshape(batch_size, kv_local, head_dim)
    new_values = project(normed, w_value).reshape(batch_size, kv_local, head_dim)
    queries = (rope_rotate(queries, lengths) * 0.0625).astype(jnp.bfloat16)
    new_keys = rope_rotate(new_keys, lengths).astype(jnp.bfloat16)
    write_slots = lengths % slots_total if is_local else lengths
    key_cache = write_slot(key_cache, new_keys, write_slots)
    value_cache = write_slot(value_cache, new_values, write_slots)
    attn_mixed = cache_attention(queries, key_cache, value_cache, lengths, is_local)
    attn_out = lax.psum(project(attn_mixed, w_out), "tp")
    hidden = (hidden.astype(jnp.float32) + rms_norm(attn_out, layer_gains[1]).astype(jnp.float32)).astype(jnp.bfloat16)
    normed = rms_norm(hidden, layer_gains[2])
    gate_proj = project(normed, w_gate)
    up_proj = project(normed, w_up)
    activated = (jax.nn.gelu(gate_proj.astype(jnp.float32), approximate=True) * up_proj.astype(jnp.float32)).astype(jnp.bfloat16)
    mlp_out = lax.psum(project(activated, w_down), "tp")
    hidden = (hidden.astype(jnp.float32) + rms_norm(mlp_out, layer_gains[3]).astype(jnp.float32)).astype(jnp.bfloat16)
    return hidden, new_keys.reshape(batch_size, kv_local * head_dim), new_values.reshape(batch_size, kv_local * head_dim)


def device_step(tokens, lengths, embed_block, norm_gains, w_query, w_key, w_value, w_out, w_gate, w_up, w_down, key_local, value_local, key_global, value_global):
    vocab_local, model_dim = embed_block.shape
    local_ids = tokens - lax.axis_index("tp") * vocab_local
    inside = (local_ids >= 0) & (local_ids < vocab_local)
    picked = jnp.take(embed_block, jnp.clip(local_ids, 0, vocab_local - 1), axis=0)
    normalizer = jnp.asarray(math.sqrt(model_dim), dtype=jnp.bfloat16).astype(jnp.float32)
    scaled = jnp.where(inside[:, None], picked.astype(jnp.float32) * normalizer, 0.0).astype(jnp.bfloat16)
    hidden = lax.psum(scaled, "tp")
    layer_weights = (w_query, w_key, w_value, w_out, w_gate, w_up, w_down)
    local_weights = tuple(weight[0] for weight in layer_weights)
    global_weights = tuple(weight[1] for weight in layer_weights)
    hidden, keys_zero, values_zero = decoder_layer(hidden, lengths, norm_gains[0:4], local_weights, key_local, value_local, True)
    hidden, keys_one, values_one = decoder_layer(hidden, lengths, norm_gains[4:8], global_weights, key_global, value_global, False)
    final_normed = rms_norm(hidden, norm_gains[8])
    raw_logits = lax.dot_general(final_normed, embed_block, (((1,), (1,)), ((), ())), preferred_element_type=jnp.float32)
    logits = 30.0 * jnp.tanh(raw_logits / 30.0)
    return logits, jnp.stack([keys_zero, keys_one]), jnp.stack([values_zero, values_one])


def solution(mesh):
    cache_spec = P("dp", None, "tp", None)
    col_spec = P(None, None, "tp")
    row_spec = P(None, "tp", None)
    rows_spec = P(None, "dp", "tp")
    in_specs = (P("dp"), P("dp"), P("tp", None), P(), col_spec, col_spec, col_spec, row_spec, col_spec, col_spec, row_spec, cache_spec, cache_spec, cache_spec, cache_spec)
    out_specs = (P("dp", "tp"), rows_spec, rows_spec)
    return jax.shard_map(device_step, mesh=mesh, in_specs=in_specs, out_specs=out_specs, check_vma=False)
```

profile of v0, /device:TPU:0, one launch (start us, length us, event | category | flops | bytes accessed | tf_op | source)
XLA Modules:
  0.0 366.1 jit_solution(14759062874232324914)
XLA Ops:
  3.7 7.1 %copy.66 = bf16[4,4096,1,256]{3,1,2,0:T(8,128)(2,1)} copy(bf16[4,4096,1,256]{3,1,2,0:T(8,128)(2,1)} %param.28) | data formatting | bytes 16777216
  10.9 7.3 %copy.67 = bf16[4,4096,1,256]{3,1,2,0:T(8,128)(2,1)} copy(bf16[4,4096,1,256]{3,1,2,0:T(8,128)(2,1)} %param.29) | data formatting | bytes 16777216
  20.1 25.3 %psum.35 = bf16[4,3840]{1,0:T(4,128)(2,1)S(1)} all-reduce(bf16[4,3840]{1,0:T(4,128)(2,1)S(1)} %select_convert_fusion), channel_id=1, replica_groups=mesh['dp'=1,'tp'=8] {'tp'}, use_global_device_ids=true, to_apply=%region_0.1 | all-reduce | flops 15360 | bytes 61440 | tf_op jit(solution)/shard_map/psum | solution.py:83
  48.4 27.8 %while.4 = (s32[]{:T(128)}, bf16[4,1024,1,256]{3,1,2,0:T(8,128)(2,1)S(1)}, s32[4,4]{1,0:T(4,128)S(1)}, bf16[4,1,1,256]{3,0,2,1:T(4,128)(2,1)S(1)}, s32[]{:T(128)}, /*index=5*/s32[4]{0:T(128)S(1)}, s32[]{:T(128)}) while((s32[]{:T(128)}, bf16[4,1024,1,256]{3,1,2,0:T(8,128)(2,1)S(1)}, s32[4,4]{1,0:T(4,128)S(1)}, bf16[4,1,1,256]{3,0,2,1:T(4,128)(2,1)S(1)}, ...), condition=%wide.while_cond, body=%wide.while_body.sunk | while | flops 285 | bytes 2755 | solution.py:28
  49.0 3.2 and_reduce_fusion.8
  56.0 3.2 and_reduce_fusion.8
  63.0 3.2 and_reduce_fusion.8
  69.9 3.2 and_reduce_fusion.8
  82.0 35.4 %while.5 = (s32[]{:T(128)}, bf16[4,1024,1,256]{3,1,2,0:T(8,128)(2,1)}, s32[4,4]{1,0:T(4,128)S(1)}, bf16[4,1,1,256]{3,0,2,1:T(4,128)(2,1)S(1)}, s32[]{:T(128)}, /*index=5*/s32[4]{0:T(128)S(1)}, s32[]{:T(128)}) while((s32[]{:T(128)}, bf16[4,1024,1,256]{3,1,2,0:T(8,128)(2,1)}, s32[4,4]{1,0:T(4,128)S(1)}, bf16[4,1,1,256]{3,0,2,1:T(4,128)(2,1)S(1)}, ...), condition=%wide.while_cond.1, body=%wide.while_body.1.sunk | while | flops 285 | bytes 2755 | solution.py:28
  82.7 3.2 and_reduce_fusion.9
  91.6 3.2 and_reduce_fusion.9
  100.4 3.2 and_reduce_fusion.9
  109.3 3.2 and_reduce_fusion.9
  122.2 23.4 %psum.36 = bf16[4,3840]{1,0:T(4,128)(2,1)S(1)} all-reduce(bf16[4,3840]{1,0:T(4,128)(2,1)S(1)} %convolution_convert_fusion.1), channel_id=1, replica_groups=mesh['dp'=1,'tp'=8] {'tp'}, use_global_device_ids=true, to_apply=%region_6.7 | all-reduce | flops 15360 | bytes 61440 | tf_op jit(solution)/shard_map/psum | solution.py:65
  146.0 6.4 %fusion.200 = f32[4,1920]{1,0:T(4,128)S(1)} fusion(bf16[2,3840,1920]{2,1,0:T(8,128)(2,1)} %param.23, bf16[4,3840]{1,0:T(4,128)(2,1)S(1)} %get-tuple-element.99, f32[3840]{0:T(1024)S(1)} %get-tuple-element.56, f32[4]{0:T(128)S(1)} %add_rsqrt_fusion.6), kind=kOutput, calls=%fused_computation.172 | convolution fusion | flops 59120640 | bytes 14822416 | tf_op jit(solution)/shard_map/dot_general | solution.py:49
  152.4 11.7 %fusion.28 = bf16[4,3840]{1,0:T(4,128)(2,1)S(1)} fusion(bf16[2,1920,3840]{2,1,0:T(8,128)(2,1)} %param.25, f32[4,1920]{1,0:T(4,128)S(1)} %fusion.200, bf16[2,3840,1920]{2,1,0:T(8,128)(2,1)} %param.24, bf16[4,3840]{1,0:T(4,128)(2,1)S(1)} %get-tuple-element.99, f32[3840]{0:T(1024)S(1)} %get-tuple-element.56, f32[4]{0:T(128)S(1)} %add_rsqrt_fusion.6), kind=kOutput, calls=%fused_computation.42 | convolution fusion | flops 118072320 | bytes 29598736 | tf_op jit(solution)/shard_map/dot_general | solution.py:49
  164.1 24.4 %psum.37 = bf16[4,3840]{1,0:T(4,128)(2,1)S(1)} all-reduce(bf16[4,3840]{1,0:T(4,128)(2,1)S(1)} %fusion.28), channel_id=1, replica_groups=mesh['dp'=1,'tp'=8] {'tp'}, use_global_device_ids=true, to_apply=%region_9.10 | all-reduce | flops 15360 | bytes 61440 | tf_op jit(solution)/shard_map/psum | solution.py:71
  191.8 35.7 %while.6 = (s32[]{:T(128)}, bf16[4,4096,1,256]{3,1,2,0:T(8,128)(2,1)}, s32[4,4]{1,0:T(4,128)S(1)}, bf16[4,1,1,256]{3,0,2,1:T(4,128)(2,1)S(1)}, s32[]{:T(128)}, /*index=5*/s32[4]{0:T(128)S(1)}, s32[]{:T(128)}) while((s32[]{:T(128)}, bf16[4,4096,1,256]{3,1,2,0:T(8,128)(2,1)}, s32[4,4]{1,0:T(4,128)S(1)}, bf16[4,1,1,256]{3,0,2,1:T(4,128)(2,1)S(1)}, ...), condition=%wide.while_cond.2, body=%wide.while_body.2.sunk | while | flops 285 | bytes 2755 | solution.py:28
  192.4 3.2 and_reduce_fusion.10
  201.3 3.2 and_reduce_fusion.10
  210.3 3.2 and_reduce_fusion.10
  219.2 3.2 and_reduce_fusion.10
  230.4 5.8 %fusion.43 = f32[4,2,4096]{2,1,0:T(2,128)S(1)} fusion(bf16[4,4096,1,256]{3,1,2,0:T(8,128)(2,1)} %get-tuple-element.24, pred[4,4096]{1,0:T(4,128)(4,1)S(1)} %iota_compare_fusion, f32[4,2,128]{2,1,0:T(2,128)S(1)} %get-tuple-element.119, f32[4,2,128]{2,1,0:T(2,128)S(1)} %get-tuple-element.118), kind=kOutput, calls=%fused_computation.49 | convolution fusion | flops 16881664 | bytes 8544256 | tf_op jit(solution)/shard_map/bkgd,bskd->bkgs/dot_general | solution.py:36
  236.8 35.1 %while.7 = (s32[]{:T(128)}, bf16[4,4096,1,256]{3,1,2,0:T(8,128)(2,1)}, s32[4,4]{1,0:T(4,128)S(1)}, bf16[4,1,1,256]{3,0,2,1:T(4,128)(2,1)S(1)}, s32[]{:T(128)}, /*index=5*/s32[4]{0:T(128)S(1)}, s32[]{:T(128)}) while((s32[]{:T(128)}, bf16[4,4096,1,256]{3,1,2,0:T(8,128)(2,1)}, s32[4,4]{1,0:T(4,128)S(1)}, bf16[4,1,1,256]{3,0,2,1:T(4,128)(2,1)S(1)}, ...), condition=%wide.while_cond.3, body=%wide.while_body.3.sunk | while | flops 285 | bytes 2755 | solution.py:28
  237.5 3.1 and_reduce_fusion.11
  246.3 3.1 and_reduce_fusion.11
  271.9 4.7 %fusion.134 = bf16[1,4,2,256]{3,2,1,0:T(2,128)(2,1)S(1)} fusion(bf16[4,4096,1,256]{3,1,2,0:T(8,128)(2,1)} %get-tuple-element.32, f32[4,2]{1,0:T(4,128)S(1)} %fusion.272, f32[4,2,4096]{2,1,0:T(2,128)S(1)} %fusion.43), kind=kOutput, calls=%fused_computation.98 | convolution fusion | flops 16881672 | bytes 8523808 | tf_op jit(solution)/shard_map/bkgs,bskd->bkgd/dot_general | solution.py:44
  279.3 23.4 %psum.38 = bf16[4,3840]{1,0:T(4,128)(2,1)S(1)} all-reduce(bf16[4,3840]{1,0:T(4,128)(2,1)S(1)} %convolution_convert_fusion), channel_id=1, replica_groups=mesh['dp'=1,'tp'=8] {'tp'}, use_global_device_ids=true, to_apply=%region_16.17 | all-reduce | flops 15360 | bytes 61440 | tf_op jit(solution)/shard_map/psum | solution.py:65
  303.1 6.4 %fusion.209 = f32[4,1920]{1,0:T(4,128)S(1)} fusion(bf16[2,3840,1920]{2,1,0:T(8,128)(2,1)} %param.23, bf16[4,3840]{1,0:T(4,128)(2,1)S(1)} %get-tuple-element.95, f32[3840]{0:T(1024)S(1)} %get-tuple-element.52, f32[4]{0:T(128)S(1)} %add_rsqrt_fusion.2), kind=kOutput, calls=%fused_computation.179 | convolution fusion | flops 59120640 | bytes 14822416 | tf_op jit(solution)/shard_map/dot_general | solution.py:49
  309.5 11.7 %fusion.31 = bf16[4,3840]{1,0:T(4,128)(2,1)S(1)} fusion(bf16[2,1920,3840]{2,1,0:T(8,128)(2,1)} %param.25, f32[4,1920]{1,0:T(4,128)S(1)} %fusion.209, bf16[2,3840,1920]{2,1,0:T(8,128)(2,1)} %param.24, bf16[4,3840]{1,0:T(4,128)(2,1)S(1)} %get-tuple-element.95, f32[3840]{0:T(1024)S(1)} %get-tuple-element.52, f32[4]{0:T(128)S(1)} %add_rsqrt_fusion.2), kind=kOutput, calls=%fused_computation.43 | convolution fusion | flops 118072320 | bytes 29598736 | tf_op jit(solution)/shard_map/dot_general | solution.py:49
  321.2 24.3 %psum.39 = bf16[4,3840]{1,0:T(4,128)(2,1)S(1)} all-reduce(bf16[4,3840]{1,0:T(4,128)(2,1)S(1)} %fusion.31), channel_id=1, replica_groups=mesh['dp'=1,'tp'=8] {'tp'}, use_global_device_ids=true, to_apply=%region_19.20 | all-reduce | flops 15360 | bytes 61440 | tf_op jit(solution)/shard_map/psum | solution.py:71
  345.9 19.6 %fusion.25 = f32[4,6144]{1,0:T(4,128)} fusion(bf16[6144,3840]{1,0:T(8,128)(2,1)} %param.17, bf16[4,3840]{1,0:T(4,128)(2,1)S(1)} %get-tuple-element.93, f32[3840]{0:T(1024)S(1)} %get-tuple-element.51, f32[4]{0:T(128)S(1)} %add_rsqrt_fusion), kind=kOutput, calls=%fused_computation.39 | convolution fusion | flops 188854272 | bytes 47330320 | tf_op jit(solution)/shard_map/dot_general | solution.py:90
  (143 shorter events, 118.8 us)
Async XLA Ops:
  10.8 7.3 %copy-start.5 = (s32[4]{0:T(128)S(1)}, s32[4]{0:T(128)}, u32[]{:S(2)}) copy-start(s32[4]{0:T(128)} %param.15) | copy-start | bytes 52
  10.8 34.8 %copy-start.1 = (bf16[9,3840]{1,0:T(8,128)(2,1)S(1)}, bf16[9,3840]{1,0:T(8,128)(2,1)}, u32[]{:S(2)}) copy-start(bf16[9,3840]{1,0:T(8,128)(2,1)} %param.18) | copy-start | bytes 207364
  10.8 37.1 %copy-start.4 = (s32[4]{0:T(128)S(1)}, s32[4]{0:T(128)}, u32[]{:S(2)}) copy-start(s32[4]{0:T(128)} %param.16) | copy-start | bytes 52
  10.8 37.3 %copy-start.6 = (s32[3]{0:T(128)S(1)}, s32[3]{0:T(128)}, u32[]{:S(2)}) copy-start(s32[3]{0:T(128)} %constant.87.clone.1) | copy-start | bytes 40
  10.8 37.3 %copy-start.7 = (s32[3]{0:T(128)S(1)}, s32[3]{0:T(128)}, u32[]{:S(2)}) copy-start(s32[3]{0:T(128)} %constant.96.clone.1) | copy-start | bytes 40
  10.9 37.5 %copy-start = (bf16[4,1024,1,256]{3,1,2,0:T(8,128)(2,1)S(1)}, bf16[4,1024,1,256]{3,1,2,0:T(8,128)(2,1)}, u32[]{:S(2)}) copy-start(bf16[4,1024,1,256]{3,1,2,0:T(8,128)(2,1)} %param.26) | copy-start | bytes 6291460
  10.9 37.5 %copy-start.3 = (s32[4]{0:T(128)S(1)}, s32[4]{0:T(128)}, u32[]{:S(2)}) copy-start(s32[4]{0:T(128)} %constant.390) | copy-start | bytes 52
  152.4 39.4 %copy-start.2 = (s32[4]{0:T(128)S(1)}, s32[4]{0:T(128)}, u32[]{:S(2)}) copy-start(s32[4]{0:T(128)} %constant.414) | copy-start | bytes 52
  230.2 6.2 %copy-start.8 = (bf16[2,3840,256]{2,1,0:T(8,128)(2,1)S(1)}, bf16[2,3840,256]{2,1,0:T(8,128)(2,1)}, u32[]{:S(2)}) copy-start(bf16[2,3840,256]{2,1,0:T(8,128)(2,1)} %param.21) | copy-start | bytes 11796484
where the time goes:
time: 369 us; the launch traced here: 366 us
  blocking collectives  121 us (33%)
  other arithmetic  93.1 us (25%)
  matrix products  86.1 us (23%)
  local copies, waits for them, and re-layouts  65 us (18%)
    scatter x32, other arithmetic  88.5 us
    dot_general x12, matrix products, project(): jnp.dot(normed, weight, preferred_element_type=jnp.float32)  53.3 us
    psum x2, blocking collectives, decoder_layer(): mlp_out = lax.psum(project(activated, w_down), 'tp')  48.7 us
    psum x2, blocking collectives, decoder_layer(): attn_out = lax.psum(project(attn_mixed, w_out), 'tp')  46.8 us
    scatter x48, local copies, waits for them, and re-layouts  45.4 us
    psum x1, blocking collectives, device_step(): hidden = lax.psum(scaled, 'tp')  25.3 us
    dot_general x1, matrix products, device_step(): lax.dot_general(final_normed, embed_block, (((1,), (1,)), ((), ())), pref...  19.6 us
    unnamed x26, local copies, waits for them, and re-layouts  17.7 us

commit v1 on v0

v1 whole, which is shorter than its diff:
```python
import functools
import math

import jax
import jax.numpy as jnp
import numpy as np
from jax import lax
from jax.experimental import pallas as pl
from jax.experimental.pallas import tpu as pltpu
from jax.sharding import PartitionSpec as P

MESH = pl.DeviceIdType.MESH
F32, BF16 = jnp.float32, jnp.bfloat16
DIM = 3840
N_DEV = 8
RING = 12
CACHE = 5
PIECE = 768
PIECES = 5
HEAD_ROWS = 512
PER_LAYER = 16
FF_COLS = (512, 512, 512, 384)


def dot(a, b):
    return jnp.dot(a, b, preferred_element_type=F32)


def dot_t(a, b):
    return lax.dot_general(a, b, (((1,), (1,)), ((), ())), preferred_element_type=F32)


def round_bf16(v):
    return v.astype(BF16).astype(F32)


def step_kernel(len_ref, emb_ref, gains_ref, freq_ref, wq, wk, wv, wo, wg, wu, wd, table, kl, vl, kg, vg,
                logits_ref, nk_ref, nv_ref,
                ring, cbuf, recv, ring_sem, c_sem, send_sem, recv_sem):
    me = lax.axis_index("tp")
    head_chunks = table.shape[0] // HEAD_ROWS

    def col_copies(slot, src_a, src_b, off_b, base, width):
        sem = ring_sem.at[slot]
        copies = []
        if src_b is None:
            copies.append((src_a.at[pl.ds(0, 2560), pl.ds(base, width)], ring.at[slot, pl.ds(0, 2560), pl.ds(0, width)]))
            src_b, off_b = src_a, base + 256
        else:
            copies.append((src_a.at[pl.ds(0, 2560), pl.ds(base, 256)], ring.at[slot, pl.ds(0, 2560), pl.ds(0, 256)]))
            copies.append((src_b.at[pl.ds(0, 2560), pl.ds(off_b, 256)], ring.at[slot, pl.ds(0, 2560), pl.ds(256, 256)]))
        copies.append((src_a.at[pl.ds(2560, 1280), pl.ds(base, 256)], ring.at[slot, pl.ds(0, 1280), pl.ds(512, 256)]))
        copies.append((src_b.at[pl.ds(2560, 1280), pl.ds(off_b, width - 256)], ring.at[slot, pl.ds(1280, 1280), pl.ds(512, width - 256)]))
        for src, dst in copies:
            pltpu.make_async_copy(src, dst, sem).start()

    def row_copies(slot, src, row0, rows):
        for j in range(PIECES):
            pltpu.make_async_copy(src.at[pl.ds(row0, rows), pl.ds(PIECE * j, PIECE)],
                                  ring.at[slot, pl.ds(rows * j, rows)], ring_sem.at[slot]).start()

    def issue(i):
        if i >= 2 * PER_LAYER + head_chunks:
            return
        slot = i % RING
        if i >= 2 * PER_LAYER:
            row_copies(slot, table, (i - 2 * PER_LAYER) * HEAD_ROWS, HEAD_ROWS)
            return
        layer, c = divmod(i, PER_LAYER)
        if c == 0:
            col_copies(slot, wq.at[layer], None, 0, 0, 512)
        elif c == 1:
            col_copies(slot, wk.at[layer], wv.at[layer], 0, 0, 512)
        elif c == 2:
            row_copies(slot, wo.at[layer], 0, 512)
        elif c < 11:
            block, which = divmod(c - 3, 2)
            col_copies(slot, (wg, wu)[which].at[layer], None, 0, 512 * block, FF_COLS[block])
        else:
            pltpu.make_async_copy(wd.at[layer, :, pl.ds(PIECE * (c - 11), PIECE)],
                                  ring.at[slot, pl.ds(0, 1920)], ring_sem.at[slot]).start()

    def arrive(i, rows=2560):
        slot = i % RING
        part = ring.at[slot] if rows == 2560 else ring.at[slot, pl.ds(0, rows)]
        pltpu.make_async_copy(part, part, ring_sem.at[slot]).wait()
        return slot

    cache_list = [kl, vl] + [kg.at[b] for b in range(4)] + [vg.at[b] for b in range(4)]

    def issue_cache(i):
        if i < len(cache_list):
            pltpu.make_async_copy(cache_list[i], cbuf.at[i % CACHE], c_sem.at[i % CACHE]).start()

    def arrive_cache(i):
        pltpu.make_async_copy(cache_list[i], cbuf.at[i % CACHE], c_sem.at[i % CACHE]).wait()
        return i % CACHE

    issue(0)
    issue(1)
    issue_cache(0)
    issue_cache(1)
    for i in range(2, RING):
        issue(i)
    for i in range(2, CACHE):
        issue_cache(i)

    barrier = pltpu.get_barrier_semaphore()
    for k in range(1, N_DEV):
        pl.semaphore_signal(barrier, inc=1, device_id={"tp": lax.rem(me + k, N_DEV)}, device_id_type=MESH)
    pl.semaphore_wait(barrier, N_DEV - 1)

    def send(step, piece=None):
        block = recv.at[step, me] if piece is None else recv.at[step, me, piece]
        for k in (7, 6, 5, 4, 3, 2, 1):
            pltpu.make_async_remote_copy(src_ref=block, dst_ref=block, send_sem=send_sem.at[step], recv_sem=recv_sem.at[step],
                                         device_id={"tp": lax.rem(me + k, N_DEV)}, device_id_type=MESH).start()

    row = lax.broadcasted_iota(jnp.int32, (8, 128), 0)
    low_rows = row < 4
    req = jnp.where(low_rows, row, row - 4)

    def tile_to(mask, width):
        return jnp.concatenate([mask] * (width // 128), axis=1) if width > 128 else mask

    low_384 = lax.broadcasted_iota(jnp.int32, (8, 384), 0) < 4
    low_256 = lax.broadcasted_iota(jnp.int32, (8, 256), 0) < 4

    def pack(value):
        return jnp.where(low_384, value[:, :384], value[:, 384:]).astype(BF16)

    def collect(step):
        whole = recv.at[step, pl.ds(0, N_DEV - 1)]
        pltpu.make_async_copy(whole, whole, recv_sem.at[step]).wait()
        parts = []
        for piece in range(PIECES):
            total = recv[step, 0, piece].astype(F32)
            for dev in range(1, N_DEV):
                total = total + recv[step, dev, piece].astype(F32)
            total = round_bf16(total)
            other = pltpu.roll(total, 4, 0)
            parts += [jnp.where(low_384, total, other), jnp.where(low_384, other, total)]
        return jnp.concatenate(parts, axis=1)

    recv[0, me] = emb_ref[...]
    send(0)

    len_row = jnp.full((8, 128), len_ref[3], jnp.int32)
    for b in range(3):
        len_row = jnp.where(req == b, len_ref[b], len_row)
    angle = len_row.astype(F32) * freq_ref[...]
    cos_tab, sin_tab = jnp.cos(angle), jnp.sin(angle)
    len_col = len_row[:, :1]

    def rotate(head):
        lo, hi = head[:, :128], head[:, 128:]
        return jnp.concatenate([lo * cos_tab - hi * sin_tab, hi * cos_tab + lo * sin_tab], axis=1)

    def norm(value, index):
        gain = gains_ref[pl.ds(index, 1), :].astype(F32)
        inv = lax.rsqrt(jnp.mean(value * value, axis=-1, keepdims=True) + 1e-6)
        return (value * inv * (1.0 + gain)).astype(BF16)

    def dot_cols(x, slot, width):
        head, tail = x[:, :2560], x[:, 2560:]
        main = dot(head, ring[slot, :, pl.ds(0, width)])
        left = dot(tail, ring[slot, pl.ds(0, 1280), pl.ds(512, 256)])
        right = dot(tail, ring[slot, pl.ds(1280, 1280), pl.ds(512, width - 256)])
        return main + jnp.concatenate([left, right], axis=1)

    def cap(scores):
        return 50.0 * jnp.tanh(scores / 50.0)

    def finish_attention(q8, scores, new_k, slots, is_local):
        slot_id = lax.broadcasted_iota(jnp.int32, (8, slots), 1)
        valid = slot_id <= len_col
        write = len_col
        if is_local:
            valid = valid | (len_col >= slots - 1)
            write = lax.rem(len_col, slots)
        valid = valid & (slot_id != write)
        capped = jnp.where(valid, cap(scores), -1e30)
        own = cap(jnp.sum(q8.astype(F32) * new_k.astype(F32), axis=-1, keepdims=True))
        top = jnp.maximum(jnp.max(capped, axis=-1, keepdims=True), own)
        grown, own = jnp.exp(capped - top), jnp.exp(own - top)
        total = jnp.sum(grown, axis=-1, keepdims=True) + own
        return (grown / total).astype(BF16), round_bf16(own / total)

    def layer_step(layer, x, is_local):
        base = PER_LAYER * layer
        a = norm(x, 4 * layer)
        slot = arrive(base)
        q = round_bf16(dot_cols(a, slot, 512))
        issue(base + RING)
        slot = arrive(base + 1)
        kv = dot_cols(a, slot, 512).astype(BF16)
        issue(base + 1 + RING)
        new_k = rotate(kv[:, :256].astype(F32)).astype(BF16)
        new_v = kv[:, 256:]
        nk_ref[layer] = new_k[:4]
        nv_ref[layer] = new_v[:4]
        q_both = jnp.where(low_256, q[:, :256], q[:, 256:])
        q8 = (rotate(q_both) * 0.0625).astype(BF16)

        if is_local:
            slots = 1024
            every = dot_t(q8, cbuf[arrive_cache(0)])
            issue_cache(CACHE)
            req_wide = tile_to(req, slots)
            scores = every[:, 3 * slots:]
            for b in range(3):
                scores = jnp.where(req_wide == b, every[:, b * slots:(b + 1) * slots], scores)
        else:
            slots = 4096
            req_wide = tile_to(req, slots)
            scores = None
            for b in range(4):
                one = dot_t(q8, cbuf[arrive_cache(2 + b)])
                issue_cache(2 + b + CACHE)
                scores = one if scores is None else jnp.where(req_wide == b, one, scores)
        probs, own = finish_attention(q8, scores, new_k, slots, is_local)
        mixed = None
        for b in range(4):
            if is_local:
                if b == 0:
                    at = arrive_cache(1)
                one = dot(probs, cbuf[at, pl.ds(b * slots, slots)])
            else:
                one = dot(probs, cbuf[arrive_cache(6 + b)])
            mixed = one if mixed is None else jnp.where(tile_to(req, 256) == b, one, mixed)
            if is_local and b == 3:
                issue_cache(1 + CACHE)
            elif not is_local:
                issue_cache(6 + b + CACHE)
        mixed = round_bf16(mixed + own * new_v.astype(F32))
        other = pltpu.roll(mixed, 4, 0)
        mixed = jnp.concatenate([jnp.where(low_256, mixed, other), jnp.where(low_256, other, mixed)], axis=1).astype(BF16)

        step = 1 + 2 * layer
        slot = arrive(base + 2)
        for j in range(PIECES):
            recv[step, me, j] = pack(dot(mixed, ring[slot, pl.ds(512 * j, 512)]))
        send(step)
        issue(base + 2 + RING)
        x = round_bf16(x + norm(collect(step), 4 * layer + 1).astype(F32))

        a = norm(x, 4 * layer + 2)
        acts = []
        for block, width in enumerate(FF_COLS):
            rows = 2560 if width == 512 else 1920
            at = base + 3 + 2 * block
            gate = round_bf16(dot_cols(a, arrive(at, rows), width))
            issue(at + RING)
            up = round_bf16(dot_cols(a, arrive(at + 1, rows), width))
            issue(at + 1 + RING)
            acts.append((jax.nn.gelu(gate, approximate=True) * up).astype(BF16))
        act = jnp.concatenate(acts, axis=1)
        step = 2 + 2 * layer
        for j in range(PIECES):
            at = base + 11 + j
            slot = arrive(at, 1920)
            recv[step, me, j] = pack(dot(act, ring[slot, pl.ds(0, 1920)]))
            send(step, j)
            issue(at + RING)
        return round_bf16(x + norm(collect(step), 4 * layer + 3).astype(F32))

    x = collect(0)
    x = layer_step(0, x, True)
    x = layer_step(1, x, False)
    z = norm(x, 8)

    def head_step(e, carry):
        slot = lax.rem(2 * PER_LAYER + e, RING)
        pltpu.make_async_copy(ring.at[slot], ring.at[slot], ring_sem.at[slot]).wait()
        acc = dot_t(z[:, :PIECE], ring[slot, pl.ds(0, HEAD_ROWS)])
        for j in range(1, PIECES):
            acc = acc + dot_t(z[:, PIECE * j:PIECE * (j + 1)], ring[slot, pl.ds(HEAD_ROWS * j, HEAD_ROWS)])
        logits_ref[:, pl.ds(pl.multiple_of(e * HEAD_ROWS, HEAD_ROWS), HEAD_ROWS)] = 30.0 * jnp.tanh(acc[:4] / 30.0)
        return carry

    lax.fori_loop(0, head_chunks, head_step, 0)

    for step in range(5):
        whole = recv.at[step, pl.ds(0, N_DEV - 1)]
        pltpu.make_async_copy(whole, whole, send_sem.at[step]).wait()


def device_step(tokens, lengths, table, gains, wq, wk, wv, wo, wg, wu, wd, kl, vl, kg, vg):
    vocab_local = table.shape[0]
    local_ids = tokens - lax.axis_index("tp") * vocab_local
    inside = (local_ids >= 0) & (local_ids < vocab_local)
    picked = jnp.take(table, jnp.clip(local_ids, 0, vocab_local - 1), axis=0)
    normalizer = jnp.asarray(math.sqrt(DIM), dtype=BF16).astype(F32)
    scaled = jnp.where(inside[:, None], picked.astype(F32) * normalizer, 0.0).astype(BF16)
    emb = scaled.reshape(4, PIECES, 2, 384).transpose(1, 2, 0, 3).reshape(PIECES, 8, 384)
    freq = jnp.asarray((10000.0 ** (-2.0 * np.arange(128, dtype=np.float64) / 256)).astype(np.float32)[None])

    def flat(cache):
        return cache.transpose(0, 2, 1, 3).reshape(4, cache.shape[1], 256)

    vmem, hbm = pl.BlockSpec(memory_space=pltpu.VMEM), pl.BlockSpec(memory_space=pl.ANY)
    smem = pl.BlockSpec(memory_space=pltpu.SMEM)
    logits, nk, nv = pl.pallas_call(
        step_kernel,
        out_shape=(jax.ShapeDtypeStruct((4, vocab_local), F32), jax.ShapeDtypeStruct((2, 4, 256), BF16), jax.ShapeDtypeStruct((2, 4, 256), BF16)),
        in_specs=[smem, vmem, vmem, vmem] + [hbm] * 12,
        out_specs=(vmem, vmem, vmem),
        scratch_shapes=[
            pltpu.VMEM((RING, 2560, PIECE), BF16),
            pltpu.VMEM((CACHE, 4096, 256), BF16),
            pltpu.VMEM((5, N_DEV, PIECES, 8, 384), BF16),
            pltpu.SemaphoreType.DMA((RING,)),
            pltpu.SemaphoreType.DMA((CACHE,)),
            pltpu.SemaphoreType.DMA((5,)),
            pltpu.SemaphoreType.DMA((5,)),
        ],
        compiler_params=pltpu.CompilerParams(collective_id=0, has_side_effects=True, vmem_limit_bytes=67_000_000),
    )(lengths, emb, gains, freq, wq, wk, wv, wo, wg, wu, wd, table,
      flat(kl).reshape(-1, 256), flat(vl).reshape(-1, 256), flat(kg), flat(vg))
    return logits, nk, nv


def solution(mesh):
    cache_spec = P("dp", None, "tp", None)
    col_spec = P(None, None, "tp")
    row_spec = P(None, "tp", None)
    rows_spec = P(None, "dp", "tp")
    in_specs = (P("dp"), P("dp"), P("tp", None), P(), col_spec, col_spec, col_spec, row_spec, col_spec, col_spec, row_spec,
                cache_spec, cache_spec, cache_spec, cache_spec)
    out_specs = (P("dp", "tp"), rows_spec, rows_spec)
    return jax.shard_map(device_step, mesh=mesh, in_specs=in_specs, out_specs=out_specs, check_vma=False)
```

time: 369 us -> 82.7 us (0.22)
  blocking collectives: 121 us -> 0 us
  other arithmetic: 93.1 us -> 0.76 us
  matrix products: 86.1 us -> 0 us
  Pallas kernels: 0 us -> 74.5 us
  local copies, waits for them, and re-layouts: 65 us -> 6.54 us
    psum x5 -> x0, blocking collectives: 121 us -> none  [the longest x2 48.7 us: decoder_layer(): mlp_out = lax.psum(project(activated, w_down), 'tp')]
    scatter x33 -> x0, other arithmetic: 88.5 us -> none
    dot_general x17 -> x0, matrix products: 86.1 us -> none  [the longest x12 53.3 us: project(): jnp.dot(normed, weight, preferred_element_type=jnp.float32)]
    pallas_call x0 -> x1, Pallas kernels: none -> 74.5 us  [device_step(): pl.pallas_call(step_kernel, out_shape=(jax.ShapeDtypeStruct((4, vocab_loc...]
    scatter x48 -> x0, local copies, waits for them, and re-layouts: 45.4 us -> none
    unnamed x26 -> x3, local copies, waits for them, and re-layouts: 17.7 us -> 4.09 us
where the time goes in v1:
time: 82.7 us; the launch traced here: 82.5 us
  Pallas kernels  74.5 us (90%)
  local copies, waits for them, and re-layouts  6.54 us (8%)
    pallas_call x1, Pallas kernels, device_step(): pl.pallas_call(step_kernel, out_shape=(jax.ShapeDtypeStruct((4, vocab_loc...  74.5 us
    unnamed x3, local copies, waits for them, and re-layouts  4.09 us
    gather x1, local copies, waits for them, and re-layouts, device_step(): picked = jnp.take(table, jnp.clip(local_ids, 0, vocab_local - 1), axis=0)  1.83 us

profile of v1, /device:TPU:0, one launch (start us, length us, event | category | flops | bytes accessed | tf_op | source)
XLA Modules:
  0.0 82.5 jit_solution(13176468874502284884)
XLA Ops:
  0.6 0.7 compare_and_fusion
  1.3 1.8 %gather_fusion = bf16[4,3840]{1,0:T(4,128)(2,1)S(1)} fusion(bf16[6144,3840]{1,0:T(8,128)(2,1)} %table.1, s32[1024]{0:T(1024)S(1)} %pad_clamp_fusion), kind=kCustom, calls=%fused_computation | custom fusion | bytes 61456 | tf_op jit(solution)/shard_map/jit(_take)/gather | solution.py:292
  3.1 0.1 fusion
  3.2 0.6 reshape.27.emb_ref
  3.9 74.5 %shard_map.175 = (f32[4,6144]{1,0:T(4,128)}, bf16[2,4,256]{2,1,0:T(4,128)(2,1)}, bf16[2,4,256]{2,1,0:T(4,128)(2,1)}) custom-call(s32[4]{0:T(128)} %len_ref.1, bf16[5,8,384]{2,1,0:T(8,128)(2,1)} %reshape.27.emb_ref, bf16[9,3840]{1,0:T(8,128)(2,1)} %gains_ref.1, f32[1,128]{1,0:T(1,128)} %constant.15.clone.freq_ref, bf16[2,3840,512]{2,1,0:T(8,128)(2,1)} %wq.1, ...), custom_call_target="tpu_custom_call" | custom-call | tf_op jit(solution)/shard_map/pallas_call | solution.py:303
  78.4 1.5 %copy.23 = f32[4,6144]{1,0:T(4,128)} copy(f32[4,6144]{1,0:T(4,128)} %get-tuple-element.9) | data formatting | bytes 196608
  80.0 1.3 %copy.24 = bf16[2,4,256]{2,1,0:T(4,128)(2,1)} copy(bf16[2,4,256]{2,1,0:T(4,128)(2,1)} %get-tuple-element.10) | data formatting | bytes 8192
  81.2 1.3 %copy.25 = bf16[2,4,256]{2,1,0:T(4,128)(2,1)} copy(bf16[2,4,256]{2,1,0:T(4,128)(2,1)} %get-tuple-element.11) | data formatting | bytes 8192
  (1 shorter events, 0.0 us)

commit v2 on v1

--- a/solution.py
+++ b/solution.py
@@ -13,8 +13,8 @@
 F32, BF16 = jnp.float32, jnp.bfloat16
 DIM = 3840
 N_DEV = 8
-RING = 12
-CACHE = 5
+RING = 10
+CACHE = 10
 PIECE = 768
 PIECES = 5
 HEAD_ROWS = 512
@@ -36,7 +36,7 @@
 
 def step_kernel(len_ref, emb_ref, gains_ref, freq_ref, wq, wk, wv, wo, wg, wu, wd, table, kl, vl, kg, vg,
                 logits_ref, nk_ref, nv_ref,
-                ring, cbuf, recv, ring_sem, c_sem, send_sem, recv_sem):
+                ring, cbuf, recv, gain_buf, freq_buf, ring_sem, c_sem, send_sem, recv_sem, small_sem):
     me = lax.axis_index("tp")
     head_chunks = table.shape[0] // HEAD_ROWS
 
@@ -89,32 +89,50 @@
     cache_list = [kl, vl] + [kg.at[b] for b in range(4)] + [vg.at[b] for b in range(4)]
 
     def issue_cache(i):
-        if i < len(cache_list):
-            pltpu.make_async_copy(cache_list[i], cbuf.at[i % CACHE], c_sem.at[i % CACHE]).start()
+        pltpu.make_async_copy(cache_list[i], cbuf.at[i], c_sem.at[i]).start()
 
     def arrive_cache(i):
-        pltpu.make_async_copy(cache_list[i], cbuf.at[i % CACHE], c_sem.at[i % CACHE]).wait()
-        return i % CACHE
+        pltpu.make_async_copy(cache_list[i], cbuf.at[i], c_sem.at[i]).wait()
+        return i
+
+    core, x_pos, y_pos = lax.rem(me, 2), lax.rem(me // 2, 2), me // 4
+    far = [(1 - y_pos, 1 - x_pos, core), (1 - y_pos, 1 - x_pos, 1 - core)]
+    near = [(y_pos, 1 - x_pos, core), (1 - y_pos, x_pos, core), (y_pos, 1 - x_pos, 1 - core), (1 - y_pos, x_pos, 1 - core)]
+    peers = [(py * 2 + px) * 2 + pc for py, px, pc in far + near + [(y_pos, x_pos, 1 - core)]]
+
+    barrier = pltpu.get_barrier_semaphore()
+    for peer in peers:
+        pl.semaphore_signal(barrier, inc=1, device_id={"tp": peer}, device_id_type=MESH)
 
     issue(0)
+    gain_copy = pltpu.make_async_copy(gains_ref, gain_buf, small_sem.at[1])
+    gain_copy.start()
+    freq_copy = pltpu.make_async_copy(freq_ref, freq_buf, small_sem.at[0])
+    freq_copy.start()
     issue(1)
-    issue_cache(0)
-    issue_cache(1)
-    for i in range(2, RING):
-        issue(i)
-    for i in range(2, CACHE):
-        issue_cache(i)
-
-    barrier = pltpu.get_barrier_semaphore()
-    for k in range(1, N_DEV):
-        pl.semaphore_signal(barrier, inc=1, device_id={"tp": lax.rem(me + k, N_DEV)}, device_id_type=MESH)
+
+    @pl.when(me >= 0)
+    def _():
+        issue_cache(0)
+        issue_cache(1)
+        issue(2)
+
+    for i in range(3, RING):
+        pl.when(me >= 0)(functools.partial(issue, i))
+
+    @pl.when(me >= 0)
+    def _():
+        for i in range(2, CACHE):
+            issue_cache(i)
+
+    recv[0, me] = emb_ref[...]
     pl.semaphore_wait(barrier, N_DEV - 1)
 
     def send(step, piece=None):
         block = recv.at[step, me] if piece is None else recv.at[step, me, piece]
-        for k in (7, 6, 5, 4, 3, 2, 1):
+        for peer in peers:
             pltpu.make_async_remote_copy(src_ref=block, dst_ref=block, send_sem=send_sem.at[step], recv_sem=recv_sem.at[step],
-                                         device_id={"tp": lax.rem(me + k, N_DEV)}, device_id_type=MESH).start()
+                                         device_id={"tp": peer}, device_id_type=MESH).start()
 
     row = lax.broadcasted_iota(jnp.int32, (8, 128), 0)
     low_rows = row < 4
@@ -142,13 +160,14 @@
             parts += [jnp.where(low_384, total, other), jnp.where(low_384, other, total)]
         return jnp.concatenate(parts, axis=1)
 
-    recv[0, me] = emb_ref[...]
     send(0)
+    gain_copy.wait()
+    freq_copy.wait()
 
     len_row = jnp.full((8, 128), len_ref[3], jnp.int32)
     for b in range(3):
         len_row = jnp.where(req == b, len_ref[b], len_row)
-    angle = len_row.astype(F32) * freq_ref[...]
+    angle = len_row.astype(F32) * freq_buf[...]
     cos_tab, sin_tab = jnp.cos(angle), jnp.sin(angle)
     len_col = len_row[:, :1]
 
@@ -157,7 +176,7 @@
         return jnp.concatenate([lo * cos_tab - hi * sin_tab, hi * cos_tab + lo * sin_tab], axis=1)
 
     def norm(value, index):
-        gain = gains_ref[pl.ds(index, 1), :].astype(F32)
+        gain = gain_buf[pl.ds(index, 1), :].astype(F32)
         inv = lax.rsqrt(jnp.mean(value * value, axis=-1, keepdims=True) + 1e-6)
         return (value * inv * (1.0 + gain)).astype(BF16)
 
@@ -205,7 +224,6 @@
         if is_local:
             slots = 1024
             every = dot_t(q8, cbuf[arrive_cache(0)])
-            issue_cache(CACHE)
             req_wide = tile_to(req, slots)
             scores = every[:, 3 * slots:]
             for b in range(3):
@@ -216,7 +234,6 @@
             scores = None
             for b in range(4):
                 one = dot_t(q8, cbuf[arrive_cache(2 + b)])
-                issue_cache(2 + b + CACHE)
                 scores = one if scores is None else jnp.where(req_wide == b, one, scores)
         probs, own = finish_attention(q8, scores, new_k, slots, is_local)
         mixed = None
@@ -228,10 +245,6 @@
             else:
                 one = dot(probs, cbuf[arrive_cache(6 + b)])
             mixed = one if mixed is None else jnp.where(tile_to(req, 256) == b, one, mixed)
-            if is_local and b == 3:
-                issue_cache(1 + CACHE)
-            elif not is_local:
-                issue_cache(6 + b + CACHE)
         mixed = round_bf16(mixed + own * new_v.astype(F32))
         other = pltpu.roll(mixed, 4, 0)
         mixed = jnp.concatenate([jnp.where(low_256, mixed, other), jnp.where(low_256, other, mixed)], axis=1).astype(BF16)
@@ -276,6 +289,11 @@
         for j in range(1, PIECES):
             acc = acc + dot_t(z[:, PIECE * j:PIECE * (j + 1)], ring[slot, pl.ds(HEAD_ROWS * j, HEAD_ROWS)])
         logits_ref[:, pl.ds(pl.multiple_of(e * HEAD_ROWS, HEAD_ROWS), HEAD_ROWS)] = 30.0 * jnp.tanh(acc[:4] / 30.0)
+
+        @pl.when(e < head_chunks - RING)
+        def _():
+            row_copies(slot, table, pl.multiple_of((e + RING) * HEAD_ROWS, HEAD_ROWS), HEAD_ROWS)
+
         return carry
 
     lax.fori_loop(0, head_chunks, head_step, 0)
@@ -285,39 +303,83 @@
         pltpu.make_async_copy(whole, whole, send_sem.at[step]).wait()
 
 
+def embed_kernel(token_ref, table, out_ref, block, sem):
+    rows = table.shape[0]
+    first = lax.axis_index("tp") * rows
+    ids, copies = [], []
+    for b in range(4):
+        local = token_ref[b] - first
+        safe = jnp.clip(local, 0, rows - 1)
+        base = pl.multiple_of((safe // 8) * 8, 8)
+        copy = pltpu.make_async_copy(table.at[pl.ds(base, 8)], block.at[b], sem.at[b])
+        copy.start()
+        copies.append(copy)
+        ids.append(jnp.where((local >= 0) & (local < rows), safe - base, -1))
+    row = lax.broadcasted_iota(jnp.int32, (8, DIM), 0)
+    scale = float(np.asarray(math.sqrt(DIM), np.float32).astype(BF16))
+    full = jnp.zeros((8, DIM), F32)
+    for b in range(4):
+        copies[b].wait()
+        mine = jnp.sum(jnp.where(row == ids[b], block[b].astype(F32), 0.0), axis=0, keepdims=True)
+        full = jnp.where((row == b) | (row == b + 4), mine * scale, full)
+    low = lax.broadcasted_iota(jnp.int32, (8, 384), 0) < 4
+    for j in range(PIECES):
+        out_ref[j] = jnp.where(low, full[:, PIECE * j:PIECE * j + 384], full[:, PIECE * j + 384:PIECE * (j + 1)]).astype(BF16)
+
+
+def pass_kernel(a_in, b_in, c_in, a_out, b_out, c_out, sem):
+    copies = [pltpu.make_async_copy(src, dst, sem.at[i]) for i, (src, dst) in enumerate(((a_in, a_out), (b_in, b_out), (c_in, c_out)))]
+    for copy in copies:
+        copy.start()
+    for copy in copies:
+        copy.wait()
+
+
 def device_step(tokens, lengths, table, gains, wq, wk, wv, wo, wg, wu, wd, kl, vl, kg, vg):
     vocab_local = table.shape[0]
-    local_ids = tokens - lax.axis_index("tp") * vocab_local
-    inside = (local_ids >= 0) & (local_ids < vocab_local)
-    picked = jnp.take(table, jnp.clip(local_ids, 0, vocab_local - 1), axis=0)
-    normalizer = jnp.asarray(math.sqrt(DIM), dtype=BF16).astype(F32)
-    scaled = jnp.where(inside[:, None], picked.astype(F32) * normalizer, 0.0).astype(BF16)
-    emb = scaled.reshape(4, PIECES, 2, 384).transpose(1, 2, 0, 3).reshape(PIECES, 8, 384)
+    vmem, hbm = pl.BlockSpec(memory_space=pltpu.VMEM), pl.BlockSpec(memory_space=pl.ANY)
+    smem = pl.BlockSpec(memory_space=pltpu.SMEM)
+    emb = pl.pallas_call(
+        embed_kernel,
+        out_shape=pltpu.VMEM((PIECES, 8, 384), BF16),
+        in_specs=[smem, hbm],
+        out_specs=vmem,
+        scratch_shapes=[pltpu.VMEM((4, 8, DIM), BF16), pltpu.SemaphoreType.DMA((4,))],
+    )(tokens, table)
     freq = jnp.asarray((10000.0 ** (-2.0 * np.arange(128, dtype=np.float64) / 256)).astype(np.float32)[None])
 
     def flat(cache):
         return cache.transpose(0, 2, 1, 3).reshape(4, cache.shape[1], 256)
 
-    vmem, hbm = pl.BlockSpec(memory_space=pltpu.VMEM), pl.BlockSpec(memory_space=pl.ANY)
-    smem = pl.BlockSpec(memory_space=pltpu.SMEM)
+    results = (jax.ShapeDtypeStruct((4, vocab_local), F32), jax.ShapeDtypeStruct((2, 4, 256), BF16), jax.ShapeDtypeStruct((2, 4, 256), BF16))
     logits, nk, nv = pl.pallas_call(
         step_kernel,
-        out_shape=(jax.ShapeDtypeStruct((4, vocab_local), F32), jax.ShapeDtypeStruct((2, 4, 256), BF16), jax.ShapeDtypeStruct((2, 4, 256), BF16)),
-        in_specs=[smem, vmem, vmem, vmem] + [hbm] * 12,
+        out_shape=tuple(pltpu.VMEM(r.shape, r.dtype) for r in results),
+        in_specs=[smem, vmem] + [hbm] * 14,
         out_specs=(vmem, vmem, vmem),
         scratch_shapes=[
             pltpu.VMEM((RING, 2560, PIECE), BF16),
             pltpu.VMEM((CACHE, 4096, 256), BF16),
             pltpu.VMEM((5, N_DEV, PIECES, 8, 384), BF16),
+            pltpu.VMEM((9, DIM), BF16),
+            pltpu.VMEM((1, 128), F32),
             pltpu.SemaphoreType.DMA((RING,)),
             pltpu.SemaphoreType.DMA((CACHE,)),
             pltpu.SemaphoreType.DMA((5,)),
             pltpu.SemaphoreType.DMA((5,)),
+            pltpu.SemaphoreType.DMA((2,)),
         ],
-        compiler_params=pltpu.CompilerParams(collective_id=0, has_side_effects=True, vmem_limit_bytes=67_000_000),
-    )(lengths, emb, gains, freq, wq, wk, wv, wo, wg, wu, wd, table,
+        compiler_params=pltpu.CompilerParams(collective_id=0, has_side_effects=True, vmem_limit_bytes=64_500_000),
+    )(lengths, pltpu.with_memory_space_constraint(emb, pltpu.VMEM), gains, freq, wq, wk, wv, wo, wg, wu, wd, table,
       flat(kl).reshape(-1, 256), flat(vl).reshape(-1, 256), flat(kg), flat(vg))
-    return logits, nk, nv
+    keep = [pltpu.with_memory_space_constraint(v, pltpu.VMEM) for v in (logits, nk, nv)]
+    return pl.pallas_call(
+        pass_kernel,
+        out_shape=results,
+        in_specs=[vmem] * 3,
+        out_specs=(hbm,) * 3,
+        scratch_shapes=[pltpu.SemaphoreType.DMA((3,))],
+    )(*keep)
 
 
 def solution(mesh):

time: 82.7 us -> 72.8 us (0.88)
  local copies, waits for them, and re-layouts: 6.54 us -> 0 us
  Pallas kernels: 74.5 us -> 71.8 us
    unnamed x3 -> x0, local copies, waits for them, and re-layouts: 4.09 us -> none
    pallas_call x1 -> x3, Pallas kernels: 74.5 us -> 71.8 us  [the longest x1 69.4 us: device_step(): pl.pallas_call(step_kernel, out_shape=tuple((pltpu.VMEM(r.shape, r.dtype)...]
    gather x1 -> x0, local copies, waits for them, and re-layouts: 1.83 us -> none  [device_step(): picked = jnp.take(table, jnp.clip(local_ids, 0, vocab_local - 1), axis=0)]
where the time goes in v2:
time: 72.8 us; the launch traced here: 72.6 us
  Pallas kernels  71.8 us (99%)
  between operations  0.81 us (1%)
    pallas_call x1, Pallas kernels, device_step(): pl.pallas_call(step_kernel, out_shape=tuple((pltpu.VMEM(r.shape, r.dtype)...  69.4 us
    pallas_call x1, Pallas kernels, device_step(): pl.pallas_call(embed_kernel, out_shape=pltpu.VMEM((PIECES, 8, 384), BF16)...  1.75 us

profile of v2, /device:TPU:0, one launch (start us, length us, event | category | flops | bytes accessed | tf_op | source)
XLA Modules:
  0.0 72.6 jit_solution(15252389464884215259)
XLA Ops:
  0.6 1.8 %shard_map.175.emb_ref = bf16[5,8,384]{2,1,0:T(8,128)(2,1)S(1)} custom-call(s32[4]{0:T(128)} %token_ref.1, bf16[6144,3840]{1,0:T(8,128)(2,1)} %table.3), custom_call_target="tpu_custom_call" | custom-call | tf_op jit(solution)/shard_map/pallas_call | solution.py:342
  2.4 69.4 %shard_map.176 = (f32[4,6144]{1,0:T(4,128)S(1)}, bf16[2,4,256]{2,1,0:T(4,128)(2,1)S(1)}, bf16[2,4,256]{2,1,0:T(4,128)(2,1)S(1)}) custom-call(s32[4]{0:T(128)} %len_ref.1, bf16[5,8,384]{2,1,0:T(8,128)(2,1)S(1)} %shard_map.175.emb_ref, bf16[9,3840]{1,0:T(8,128)(2,1)} %gains_ref.1, f32[1,128]{1,0:T(1,128)} %constant.2.clone.freq_ref, bf16[2,3840,512]{2,1,0:T(8,128)(2,1)} %wq.1, ...), custom_call_target="tpu_custom_call" | custom-call | tf_op jit(solution)/shard_map/pallas_call | solution.py:355
  71.8 0.7 shard_map.177

commit v3 on v2

--- a/solution.py
+++ b/solution.py
@@ -18,6 +18,7 @@
 PIECE = 768
 PIECES = 5
 HEAD_ROWS = 512
+HEAD_EARLY = 6
 PER_LAYER = 16
 FF_COLS = (512, 512, 512, 384)
 
@@ -35,10 +36,9 @@
 
 
 def step_kernel(len_ref, emb_ref, gains_ref, freq_ref, wq, wk, wv, wo, wg, wu, wd, table, kl, vl, kg, vg,
-                logits_ref, nk_ref, nv_ref,
-                ring, cbuf, recv, gain_buf, freq_buf, ring_sem, c_sem, send_sem, recv_sem, small_sem):
+                z_out, nk_ref, nv_ref, ring,
+                cbuf, recv, gain_buf, freq_buf, ring_sem, c_sem, send_sem, recv_sem, small_sem):
     me = lax.axis_index("tp")
-    head_chunks = table.shape[0] // HEAD_ROWS
 
     def col_copies(slot, src_a, src_b, off_b, base, width):
         sem = ring_sem.at[slot]
@@ -60,7 +60,7 @@
                                   ring.at[slot, pl.ds(rows * j, rows)], ring_sem.at[slot]).start()
 
     def issue(i):
-        if i >= 2 * PER_LAYER + head_chunks:
+        if i >= 2 * PER_LAYER + HEAD_EARLY:
             return
         slot = i % RING
         if i >= 2 * PER_LAYER:
@@ -104,27 +104,20 @@
     for peer in peers:
         pl.semaphore_signal(barrier, inc=1, device_id={"tp": peer}, device_id_type=MESH)
 
-    issue(0)
+    def start(chunks, caches=()):
+        @pl.when(me >= 0)
+        def _():
+            for i in chunks:
+                issue(i)
+            for i in caches:
+                issue_cache(i)
+
     gain_copy = pltpu.make_async_copy(gains_ref, gain_buf, small_sem.at[1])
+    freq_copy = pltpu.make_async_copy(freq_ref, freq_buf, small_sem.at[0])
+    start((0,))
     gain_copy.start()
-    freq_copy = pltpu.make_async_copy(freq_ref, freq_buf, small_sem.at[0])
     freq_copy.start()
-    issue(1)
-
-    @pl.when(me >= 0)
-    def _():
-        issue_cache(0)
-        issue_cache(1)
-        issue(2)
-
-    for i in range(3, RING):
-        pl.when(me >= 0)(functools.partial(issue, i))
-
-    @pl.when(me >= 0)
-    def _():
-        for i in range(2, CACHE):
-            issue_cache(i)
-
+    start((1,), (0, 1))
     recv[0, me] = emb_ref[...]
     pl.semaphore_wait(barrier, N_DEV - 1)
 
@@ -161,6 +154,8 @@
         return jnp.concatenate(parts, axis=1)
 
     send(0)
+    for i in range(2, RING):
+        start((i,))
     gain_copy.wait()
     freq_copy.wait()
 
@@ -186,6 +181,13 @@
         left = dot(tail, ring[slot, pl.ds(0, 1280), pl.ds(512, 256)])
         right = dot(tail, ring[slot, pl.ds(1280, 1280), pl.ds(512, width - 256)])
         return main + jnp.concatenate([left, right], axis=1)
+
+    def dot_piece(x, slot, row0, rows):
+        half = 256 * ((rows + 256) // 512)
+        left = dot(x, ring[slot, pl.ds(row0, rows), pl.ds(0, 512)])
+        one = dot(x[:, :half], ring[slot, pl.ds(row0, half), pl.ds(512, 256)])
+        two = dot(-x[:, half:], ring[slot, pl.ds(row0 + half, rows - half), pl.ds(512, 256)])
+        return jnp.concatenate([left, one - two], axis=1)
 
     def cap(scores):
         return 50.0 * jnp.tanh(scores / 50.0)
@@ -210,10 +212,9 @@
         a = norm(x, 4 * layer)
         slot = arrive(base)
         q = round_bf16(dot_cols(a, slot, 512))
-        issue(base + RING)
         slot = arrive(base + 1)
         kv = dot_cols(a, slot, 512).astype(BF16)
-        issue(base + 1 + RING)
+        start((base + RING, base + 1 + RING))
         new_k = rotate(kv[:, :256].astype(F32)).astype(BF16)
         new_v = kv[:, 256:]
         nk_ref[layer] = new_k[:4]
@@ -243,7 +244,8 @@
                     at = arrive_cache(1)
                 one = dot(probs, cbuf[at, pl.ds(b * slots, slots)])
             else:
-                one = dot(probs, cbuf[arrive_cache(6 + b)])
+                at = arrive_cache(6 + b)
+                one = dot(probs[:, :2048], cbuf[at, pl.ds(0, 2048)]) - dot(-probs[:, 2048:], cbuf[at, pl.ds(2048, 2048)])
             mixed = one if mixed is None else jnp.where(tile_to(req, 256) == b, one, mixed)
         mixed = round_bf16(mixed + own * new_v.astype(F32))
         other = pltpu.roll(mixed, 4, 0)
@@ -252,9 +254,9 @@
         step = 1 + 2 * layer
         slot = arrive(base + 2)
         for j in range(PIECES):
-            recv[step, me, j] = pack(dot(mixed, ring[slot, pl.ds(512 * j, 512)]))
-        send(step)
-        issue(base + 2 + RING)
+            recv[step, me, j] = pack(dot_piece(mixed, slot, 512 * j, 512))
+            send(step, j)
+        start((base + 2 + RING,))
         x = round_bf16(x + norm(collect(step), 4 * layer + 1).astype(F32))
 
         a = norm(x, 4 * layer + 2)
@@ -262,41 +264,28 @@
         for block, width in enumerate(FF_COLS):
             rows = 2560 if width == 512 else 1920
             at = base + 3 + 2 * block
-            gate = round_bf16(dot_cols(a, arrive(at, rows), width))
-            issue(at + RING)
-            up = round_bf16(dot_cols(a, arrive(at + 1, rows), width))
-            issue(at + 1 + RING)
+            gate_slot, up_slot = arrive(at, rows), arrive(at + 1, rows)
+            gate = round_bf16(dot_cols(a, gate_slot, width))
+            up = round_bf16(dot_cols(a, up_slot, width))
+            start((at + RING, at + 1 + RING), (2 + 2 * block, 3 + 2 * block) if is_local else ())
             acts.append((jax.nn.gelu(gate, approximate=True) * up).astype(BF16))
         act = jnp.concatenate(acts, axis=1)
         step = 2 + 2 * layer
         for j in range(PIECES):
             at = base + 11 + j
             slot = arrive(at, 1920)
-            recv[step, me, j] = pack(dot(act, ring[slot, pl.ds(0, 1920)]))
+            recv[step, me, j] = pack(dot_piece(act, slot, 0, 1920))
             send(step, j)
-            issue(at + RING)
+            start((at + RING,))
         return round_bf16(x + norm(collect(step), 4 * layer + 3).astype(F32))
 
     x = collect(0)
     x = layer_step(0, x, True)
     x = layer_step(1, x, False)
     z = norm(x, 8)
-
-    def head_step(e, carry):
-        slot = lax.rem(2 * PER_LAYER + e, RING)
-        pltpu.make_async_copy(ring.at[slot], ring.at[slot], ring_sem.at[slot]).wait()
-        acc = dot_t(z[:, :PIECE], ring[slot, pl.ds(0, HEAD_ROWS)])
-        for j in range(1, PIECES):
-            acc = acc + dot_t(z[:, PIECE * j:PIECE * (j + 1)], ring[slot, pl.ds(HEAD_ROWS * j, HEAD_ROWS)])
-        logits_ref[:, pl.ds(pl.multiple_of(e * HEAD_ROWS, HEAD_ROWS), HEAD_ROWS)] = 30.0 * jnp.tanh(acc[:4] / 30.0)
-
-        @pl.when(e < head_chunks - RING)
-        def _():
-            row_copies(slot, table, pl.multiple_of((e + RING) * HEAD_ROWS, HEAD_ROWS), HEAD_ROWS)
-
-        return carry
-
-    lax.fori_loop(0, head_chunks, head_step, 0)
+    z_out[...] = jnp.concatenate([z, z], axis=0)
+    for i in range(HEAD_EARLY):
+        arrive(2 * PER_LAYER + i)
 
     for step in range(5):
         whole = recv.at[step, pl.ds(0, N_DEV - 1)]
@@ -327,11 +316,99 @@
         out_ref[j] = jnp.where(low, full[:, PIECE * j:PIECE * j + 384], full[:, PIECE * j + 384:PIECE * (j + 1)]).astype(BF16)
 
 
-def pass_kernel(a_in, b_in, c_in, a_out, b_out, c_out, sem):
-    copies = [pltpu.make_async_copy(src, dst, sem.at[i]) for i, (src, dst) in enumerate(((a_in, a_out), (b_in, b_out), (c_in, c_out)))]
-    for copy in copies:
+def head_kernel(z_ref, early, nk_in, nv_in, table, logits_out, nk_out, nv_out, late, turned, logits_ref, late_sem, out_sem):
+    chunks = table.shape[0] // HEAD_ROWS
+    pairs, depth = chunks // 2, DIM // 256
+    for i in range(chunks - HEAD_EARLY):
+        for j in range(PIECES):
+            pltpu.make_async_copy(table.at[pl.ds((HEAD_EARLY + i) * HEAD_ROWS, HEAD_ROWS), pl.ds(PIECE * j, PIECE)],
+                                  late.at[i, pl.ds(HEAD_ROWS * j, HEAD_ROWS)], late_sem.at[i]).start()
+    keep = [pltpu.make_async_copy(nk_in, nk_out, out_sem.at[0]), pltpu.make_async_copy(nv_in, nv_out, out_sem.at[1])]
+    for copy in keep:
         copy.start()
-    for copy in copies:
+
+    turned[:, pl.ds(128, 128)] = jnp.zeros((DIM, 128), BF16)
+    for j in range(DIM // 128):
+        block = jnp.concatenate([z_ref[:, pl.ds(128 * j, 128)].astype(F32), jnp.zeros((112, 128), F32)], axis=0)
+        turned[pl.ds(128 * j, 128), pl.ds(0, 128)] = block.T.astype(BF16)
+
+    def part(chunk, row0, rows, c):
+        span = pl.ds(row0, rows), pl.ds(256 * c, 256)
+        if chunk < HEAD_EARLY:
+            return early[(2 * PER_LAYER + chunk) % RING, span[0], span[1]]
+        return late[chunk - HEAD_EARLY, span[0], span[1]]
+
+    def unit(q, acc_a, acc_b, need):
+        order = [(p, k) for p in range(pairs) for k in range((q + p) % 2, depth, 2)]
+
+        def push(value, register, transpose=False):
+            pltpu.matmul_push_rhs(value, staging_register=register, mxu_index=q, transpose=transpose)
+
+        def weights(p, k, half):
+            return part(2 * p, HEAD_ROWS * (k // 3) + 256 * half, 256, k % 3)
+
+        def turned_block(k):
+            return turned[pl.ds(256 * k, 256), :]
+
+        one, two = 0, 1
+        push(weights(*order[0], 0), one, True)
+        push(turned_block(order[0][1]), two)
+        yield None
+        for n, (p, k) in enumerate(order):
+            lhs = z_ref[:, pl.ds(256 * k, 256)]
+            following = order[n + 1] if n + 1 < len(order) else None
+            pltpu.matmul_acc_lhs(acc_a[p % 2][0], lhs, load_staged_rhs=one)
+            push(weights(p, k, 1), one, True)
+            if n and order[n - 1][0] < p:
+                yield p - 1
+            pltpu.matmul_acc_lhs(acc_b, part(2 * p + 1, HEAD_ROWS * (k // 3), HEAD_ROWS, k % 3), load_staged_rhs=two)
+            if following:
+                need(following[0])
+                push(weights(*following, 0), two, True)
+            pltpu.matmul_acc_lhs(acc_a[p % 2][1], lhs, load_staged_rhs=one)
+            if following:
+                push(turned_block(following[1]), one)
+            one, two = two, one
+            yield None
+        yield pairs - 1
+
+    def run(*accs):
+        acc_a, acc_b = ((accs[0:2], accs[2:4]), (accs[4:6], accs[6:8])), accs[8:]
+        for acc in accs:
+            pltpu.matmul_pop(acc)
+        waited = set()
+
+        def need(p):
+            for chunk in (2 * p, 2 * p + 1):
+                if chunk >= HEAD_EARLY and chunk not in waited:
+                    waited.add(chunk)
+                    i = chunk - HEAD_EARLY
+                    pltpu.make_async_copy(late.at[i], late.at[i], late_sem.at[i]).wait()
+
+        def write(chunk, value):
+            logits_ref[:, pl.ds(chunk * HEAD_ROWS, HEAD_ROWS)] = 30.0 * jnp.tanh(value[:4] / 30.0)
+
+        running = {q: unit(q, acc_a[q], acc_b[q], need) for q in range(2)}
+        half_done = {}
+        while running:
+            for q in list(running):
+                p = next(running[q], "end")
+                if p == "end":
+                    del running[q]
+                elif p is not None:
+                    popped = [pltpu.matmul_pop(acc_b[q])[:, :128]] + [pltpu.matmul_pop(acc) for acc in acc_a[q][p % 2]]
+                    if p not in half_done:
+                        half_done[p] = popped
+                        continue
+                    tall, left, right = [x + y for x, y in zip(popped, half_done.pop(p))]
+                    write(2 * p, jnp.concatenate([left, right], axis=1))
+                    write(2 * p + 1, jnp.concatenate([tall[128 * t:128 * (t + 1)].T[:8] for t in range(4)], axis=1))
+
+    pl.run_scoped(run, *[pltpu.ACC(q)((16, 256), F32) for q in (0, 0, 0, 0, 1, 1, 1, 1)],
+                  *[pltpu.ACC(q)((HEAD_ROWS, 256), F32) for q in (0, 1)])
+    final = pltpu.make_async_copy(logits_ref, logits_out, out_sem.at[2])
+    final.start()
+    for copy in keep + [final]:
         copy.wait()
 
 
@@ -348,17 +425,19 @@
     )(tokens, table)
     freq = jnp.asarray((10000.0 ** (-2.0 * np.arange(128, dtype=np.float64) / 256)).astype(np.float32)[None])
 
+    def in_vmem(value):
+        return pltpu.with_memory_space_constraint(value, pltpu.VMEM)
+
     def flat(cache):
         return cache.transpose(0, 2, 1, 3).reshape(4, cache.shape[1], 256)
 
     results = (jax.ShapeDtypeStruct((4, vocab_local), F32), jax.ShapeDtypeStruct((2, 4, 256), BF16), jax.ShapeDtypeStruct((2, 4, 256), BF16))
-    logits, nk, nv = pl.pallas_call(
+    z, nk, nv, ring = pl.pallas_call(
         step_kernel,
-        out_shape=tuple(pltpu.VMEM(r.shape, r.dtype) for r in results),
+        out_shape=(pltpu.VMEM((16, DIM), BF16),) + tuple(pltpu.VMEM(r.shape, r.dtype) for r in results[1:]) + (pltpu.VMEM((RING, 2560, PIECE), BF16),),
         in_specs=[smem, vmem] + [hbm] * 14,
-        out_specs=(vmem, vmem, vmem),
+        out_specs=(vmem,) * 4,
         scratch_shapes=[
-            pltpu.VMEM((RING, 2560, PIECE), BF16),
             pltpu.VMEM((CACHE, 4096, 256), BF16),
             pltpu.VMEM((5, N_DEV, PIECES, 8, 384), BF16),
             pltpu.VMEM((9, DIM), BF16),
@@ -369,17 +448,24 @@
             pltpu.SemaphoreType.DMA((5,)),
             pltpu.SemaphoreType.DMA((2,)),
         ],
-        compiler_params=pltpu.CompilerParams(collective_id=0, has_side_effects=True, vmem_limit_bytes=64_500_000),
-    )(lengths, pltpu.with_memory_space_constraint(emb, pltpu.VMEM), gains, freq, wq, wk, wv, wo, wg, wu, wd, table,
+        compiler_params=pltpu.CompilerParams(collective_id=0, has_side_effects=True, vmem_limit_bytes=25_000_000),
+    )(lengths, in_vmem(emb), gains, freq, wq, wk, wv, wo, wg, wu, wd, table,
       flat(kl).reshape(-1, 256), flat(vl).reshape(-1, 256), flat(kg), flat(vg))
-    keep = [pltpu.with_memory_space_constraint(v, pltpu.VMEM) for v in (logits, nk, nv)]
+    late = vocab_local // HEAD_ROWS - HEAD_EARLY
     return pl.pallas_call(
-        pass_kernel,
+        head_kernel,
         out_shape=results,
-        in_specs=[vmem] * 3,
+        in_specs=[vmem] * 4 + [hbm],
         out_specs=(hbm,) * 3,
-        scratch_shapes=[pltpu.SemaphoreType.DMA((3,))],
-    )(*keep)
+        scratch_shapes=[
+            pltpu.VMEM((late, 2560, PIECE), BF16),
+            pltpu.VMEM((DIM, 256), BF16),
+            pltpu.VMEM((4, vocab_local), F32),
+            pltpu.SemaphoreType.DMA((late,)),
+            pltpu.SemaphoreType.DMA((3,)),
+        ],
+        compiler_params=pltpu.CompilerParams(vmem_limit_bytes=27_000_000),
+    )(in_vmem(z), in_vmem(ring), in_vmem(nk), in_vmem(nv), table)
 
 
 def solution(mesh):

time: 72.8 us -> 63.4 us (0.87)
  Pallas kernels: 71.8 us -> 62.5 us
    pallas_call x2, Pallas kernels: 70.1 us -> 60.7 us  [the longest x1 50.5 us: device_step(): pl.pallas_call(step_kernel, out_shape=(pltpu.VMEM((16, DIM), BF16),) + tu...]
where the time goes in v3:
time: 63.4 us; the launch traced here: 63.3 us
  Pallas kernels  62.5 us (99%)
  between operations  0.81 us (1%)
    pallas_call x1, Pallas kernels, device_step(): pl.pallas_call(step_kernel, out_shape=(pltpu.VMEM((16, DIM), BF16),) + tu...  50.5 us
    pallas_call x1, Pallas kernels, device_step(): pl.pallas_call(head_kernel, out_shape=results, in_specs=[vmem] * 4 + [hbm...  10.3 us
    pallas_call x1, Pallas kernels, device_step(): pl.pallas_call(embed_kernel, out_shape=pltpu.VMEM((PIECES, 8, 384), BF16)...  1.75 us

profile of v3, /device:TPU:0, one launch (start us, length us, event | category | flops | bytes accessed | tf_op | source)
XLA Modules:
  0.0 63.3 jit_solution(3001108790749315161)
XLA Ops:
  0.6 1.8 %shard_map.175.emb_ref = bf16[5,8,384]{2,1,0:T(8,128)(2,1)S(1)} custom-call(s32[4]{0:T(128)} %token_ref.1, bf16[6144,3840]{1,0:T(8,128)(2,1)} %table.5), custom_call_target="tpu_custom_call" | custom-call | tf_op jit(solution)/shard_map/pallas_call | solution.py:419
  2.4 50.5 %shard_map.176 = (bf16[16,3840]{1,0:T(8,128)(2,1)S(1)}, bf16[2,4,256]{2,1,0:T(4,128)(2,1)S(1)}, bf16[2,4,256]{2,1,0:T(4,128)(2,1)S(1)}, bf16[10,2560,768]{2,1,0:T(8,128)(2,1)S(1)}) custom-call(s32[4]{0:T(128)} %len_ref.1, bf16[5,8,384]{2,1,0:T(8,128)(2,1)S(1)} %shard_map.175.emb_ref, bf16[9,3840]{1,0:T(8,128)(2,1)} %gains_ref.1, ...), custom_call_target="tpu_custom_call" | custom-call | tf_op jit(solution)/shard_map/pallas_call | solution.py:435
  52.9 10.3 %shard_map.177 = (f32[4,6144]{1,0:T(4,128)}, bf16[2,4,256]{2,1,0:T(4,128)(2,1)}, bf16[2,4,256]{2,1,0:T(4,128)(2,1)}) custom-call(bf16[16,3840]{1,0:T(8,128)(2,1)S(1)} %get-tuple-element.7.z_ref, bf16[10,2560,768]{2,1,0:T(8,128)(2,1)S(1)} %get-tuple-element.8.early, bf16[2,4,256]{2,1,0:T(4,128)(2,1)S(1)} %get-tuple-element.9.nk_in, ...), custom_call_target="tpu_custom_call" | custom-call | tf_op jit(solution)/shard_map/pallas_call | solution.py:455

commit v4 on v3

--- a/solution.py
+++ b/solution.py
@@ -20,7 +20,7 @@
 HEAD_ROWS = 512
 HEAD_EARLY = 6
 PER_LAYER = 16
-FF_COLS = (512, 512, 512, 384)
+FF_ROWS = (1024, 1024, 1024, 768)
 
 
 def dot(a, b):
@@ -75,7 +75,12 @@
             row_copies(slot, wo.at[layer], 0, 512)
         elif c < 11:
             block, which = divmod(c - 3, 2)
-            col_copies(slot, (wg, wu)[which].at[layer], None, 0, 512 * block, FF_COLS[block])
+            src, rows, row0 = (wg, wu)[which].at[layer], FF_ROWS[block], 1024 * block
+            half = rows // 2
+            for src_row, count, col, width, row, at in ((0, rows, 0, PIECE, 0, 0), (0, rows, PIECE, PIECE, rows, 0),
+                                                        (0, half, 2 * PIECE, 384, 2 * rows, 0), (half, half, 2 * PIECE, 384, 2 * rows, 384)):
+                pltpu.make_async_copy(src.at[pl.ds(row0 + src_row, count), pl.ds(col, width)],
+                                      ring.at[slot, pl.ds(row, count), pl.ds(at, width)], ring_sem.at[slot]).start()
         else:
             pltpu.make_async_copy(wd.at[layer, :, pl.ds(PIECE * (c - 11), PIECE)],
                                   ring.at[slot, pl.ds(0, 1920)], ring_sem.at[slot]).start()
@@ -181,6 +186,16 @@
         left = dot(tail, ring[slot, pl.ds(0, 1280), pl.ds(512, 256)])
         right = dot(tail, ring[slot, pl.ds(1280, 1280), pl.ds(512, width - 256)])
         return main + jnp.concatenate([left, right], axis=1)
+
+    def dot_rows(x, slot, rows):
+        half = rows // 2
+        parts = []
+        for row in (0, rows):
+            parts.append(dot(x, ring[slot, pl.ds(row, rows), pl.ds(0, 512)]))
+            parts.append(dot(x, ring[slot, pl.ds(row, rows), pl.ds(512, 256)]))
+        top, low = dot(x[:, :half], ring[slot, pl.ds(2 * rows, half), pl.ds(0, 384)]), dot(x[:, half:], ring[slot, pl.ds(2 * rows, half), pl.ds(384, 384)])
+        parts.append(top + low)
+        return parts
 
     def dot_piece(x, slot, row0, rows):
         half = 256 * ((rows + 256) // 512)
@@ -260,16 +275,17 @@
         x = round_bf16(x + norm(collect(step), 4 * layer + 1).astype(F32))
 
         a = norm(x, 4 * layer + 2)
-        acts = []
-        for block, width in enumerate(FF_COLS):
-            rows = 2560 if width == 512 else 1920
-            at = base + 3 + 2 * block
-            gate_slot, up_slot = arrive(at, rows), arrive(at + 1, rows)
-            gate = round_bf16(dot_cols(a, gate_slot, width))
-            up = round_bf16(dot_cols(a, up_slot, width))
+        gate = up = None
+        for block, rows in enumerate(FF_ROWS):
+            at, filled = base + 3 + 2 * block, 2560 * rows // 1024
+            gate_slot, up_slot = arrive(at, filled), arrive(at + 1, filled)
+            part = a[:, 1024 * block:1024 * block + rows]
+            part = part if block == 0 else -part
+            gate_part, up_part = dot_rows(part, gate_slot, rows), dot_rows(part, up_slot, rows)
+            gate = gate_part if gate is None else [x - y for x, y in zip(gate, gate_part)]
+            up = up_part if up is None else [x - y for x, y in zip(up, up_part)]
             start((at + RING, at + 1 + RING), (2 + 2 * block, 3 + 2 * block) if is_local else ())
-            acts.append((jax.nn.gelu(gate, approximate=True) * up).astype(BF16))
-        act = jnp.concatenate(acts, axis=1)
+        act = jnp.concatenate([(jax.nn.gelu(round_bf16(x), approximate=True) * round_bf16(y)).astype(BF16) for x, y in zip(gate, up)], axis=1)
         step = 2 + 2 * layer
         for j in range(PIECES):
             at = base + 11 + j
@@ -319,10 +335,11 @@
 def head_kernel(z_ref, early, nk_in, nv_in, table, logits_out, nk_out, nv_out, late, turned, logits_ref, late_sem, out_sem):
     chunks = table.shape[0] // HEAD_ROWS
     pairs, depth = chunks // 2, DIM // 256
-    for i in range(chunks - HEAD_EARLY):
+    for i in range(0, chunks - HEAD_EARLY, 2):
         for j in range(PIECES):
-            pltpu.make_async_copy(table.at[pl.ds((HEAD_EARLY + i) * HEAD_ROWS, HEAD_ROWS), pl.ds(PIECE * j, PIECE)],
-                                  late.at[i, pl.ds(HEAD_ROWS * j, HEAD_ROWS)], late_sem.at[i]).start()
+            for n in (i, i + 1):
+                pltpu.make_async_copy(table.at[pl.ds((HEAD_EARLY + n) * HEAD_ROWS, HEAD_ROWS), pl.ds(PIECE * j, PIECE)],
+                                      late.at[n, pl.ds(HEAD_ROWS * j, HEAD_ROWS)], late_sem.at[i // 2, j]).start()
     keep = [pltpu.make_async_copy(nk_in, nk_out, out_sem.at[0]), pltpu.make_async_copy(nv_in, nv_out, out_sem.at[1])]
     for copy in keep:
         copy.start()
@@ -363,7 +380,7 @@
                 yield p - 1
             pltpu.matmul_acc_lhs(acc_b, part(2 * p + 1, HEAD_ROWS * (k // 3), HEAD_ROWS, k % 3), load_staged_rhs=two)
             if following:
-                need(following[0])
+                need(*following)
                 push(weights(*following, 0), two, True)
             pltpu.matmul_acc_lhs(acc_a[p % 2][1], lhs, load_staged_rhs=one)
             if following:
@@ -378,12 +395,12 @@
             pltpu.matmul_pop(acc)
         waited = set()
 
-        def need(p):
-            for chunk in (2 * p, 2 * p + 1):
-                if chunk >= HEAD_EARLY and chunk not in waited:
-                    waited.add(chunk)
-                    i = chunk - HEAD_EARLY
-                    pltpu.make_async_copy(late.at[i], late.at[i], late_sem.at[i]).wait()
+        def need(p, k):
+            key = 2 * p - HEAD_EARLY, k // 3
+            if key[0] >= 0 and key not in waited:
+                waited.add(key)
+                both = late.at[key[0], pl.ds(0, 2 * HEAD_ROWS)]
+                pltpu.make_async_copy(both, both, late_sem.at[key[0] // 2, key[1]]).wait()
 
         def write(chunk, value):
             logits_ref[:, pl.ds(chunk * HEAD_ROWS, HEAD_ROWS)] = 30.0 * jnp.tanh(value[:4] / 30.0)
@@ -448,7 +465,7 @@
             pltpu.SemaphoreType.DMA((5,)),
             pltpu.SemaphoreType.DMA((2,)),
         ],
-        compiler_params=pltpu.CompilerParams(collective_id=0, has_side_effects=True, vmem_limit_bytes=25_000_000),
+        compiler_params=pltpu.CompilerParams(collective_id=0, has_side_effects=True, vmem_limit_bytes=26_000_000),
     )(lengths, in_vmem(emb), gains, freq, wq, wk, wv, wo, wg, wu, wd, table,
       flat(kl).reshape(-1, 256), flat(vl).reshape(-1, 256), flat(kg), flat(vg))
     late = vocab_local // HEAD_ROWS - HEAD_EARLY
@@ -461,7 +478,7 @@
             pltpu.VMEM((late, 2560, PIECE), BF16),
             pltpu.VMEM((DIM, 256), BF16),
             pltpu.VMEM((4, vocab_local), F32),
-            pltpu.SemaphoreType.DMA((late,)),
+            pltpu.SemaphoreType.DMA((late // 2, PIECES)),
             pltpu.SemaphoreType.DMA((3,)),
         ],
         compiler_params=pltpu.CompilerParams(vmem_limit_bytes=27_000_000),

time: 63.4 us -> 62.9 us (level)
  no operation moved by 1% of the time
where the time goes in v4:
time: 62.9 us; the launch traced here: 62.8 us
  Pallas kernels  62 us (99%)
  between operations  0.81 us (1%)
    pallas_call x1, Pallas kernels, device_step(): pl.pallas_call(step_kernel, out_shape=(pltpu.VMEM((16, DIM), BF16),) + tu...  50.3 us
    pallas_call x1, Pallas kernels, device_step(): pl.pallas_call(head_kernel, out_shape=results, in_specs=[vmem] * 4 + [hbm...  9.92 us
    pallas_call x1, Pallas kernels, device_step(): pl.pallas_call(embed_kernel, out_shape=pltpu.VMEM((PIECES, 8, 384), BF16)...  1.75 us

profile of v4, /device:TPU:0, one launch (start us, length us, event | category | flops | bytes accessed | tf_op | source)
XLA Modules:
  0.0 62.8 jit_solution(1104958150417054763)
XLA Ops:
  0.6 1.8 %shard_map.175.emb_ref = bf16[5,8,384]{2,1,0:T(8,128)(2,1)S(1)} custom-call(s32[4]{0:T(128)} %token_ref.1, bf16[6144,3840]{1,0:T(8,128)(2,1)} %table.5), custom_call_target="tpu_custom_call" | custom-call | tf_op jit(solution)/shard_map/pallas_call | solution.py:436
  2.4 50.3 %shard_map.176 = (bf16[16,3840]{1,0:T(8,128)(2,1)S(1)}, bf16[2,4,256]{2,1,0:T(4,128)(2,1)S(1)}, bf16[2,4,256]{2,1,0:T(4,128)(2,1)S(1)}, bf16[10,2560,768]{2,1,0:T(8,128)(2,1)S(1)}) custom-call(s32[4]{0:T(128)} %len_ref.1, bf16[5,8,384]{2,1,0:T(8,128)(2,1)S(1)} %shard_map.175.emb_ref, bf16[9,3840]{1,0:T(8,128)(2,1)} %gains_ref.1, ...), custom_call_target="tpu_custom_call" | custom-call | tf_op jit(solution)/shard_map/pallas_call | solution.py:452
  52.7 9.9 %shard_map.177 = (f32[4,6144]{1,0:T(4,128)}, bf16[2,4,256]{2,1,0:T(4,128)(2,1)}, bf16[2,4,256]{2,1,0:T(4,128)(2,1)}) custom-call(bf16[16,3840]{1,0:T(8,128)(2,1)S(1)} %get-tuple-element.7.z_ref, bf16[10,2560,768]{2,1,0:T(8,128)(2,1)S(1)} %get-tuple-element.8.early, bf16[2,4,256]{2,1,0:T(4,128)(2,1)S(1)} %get-tuple-element.9.nk_in, ...), custom_call_target="tpu_custom_call" | custom-call | tf_op jit(solution)/shard_map/pallas_call | solution.py:472
